TPU v7x, 32 devices: a whole 2x2x4 slice. The times are simulated.
32 devices in a mesh: member: 8 (over y, x, core), tensor: 4 (over z).
Axes of the slice: x: 2, y: 2, z: 4, core: 2. Of those that a mesh axis runs over, the one named last changes fastest.
Arguments:
- prompt_acts: bfloat16 [128, 5120], P(None, 'member'), may hold values from -6 to 6
- gate_weight: bfloat16 [5120, 13824], P('member', 'tensor'), may hold values from -0.078125 to 0.078125
- up_weight: bfloat16 [5120, 13824], P('member', 'tensor'), may hold values from -0.078125 to 0.078125
- down_weight: bfloat16 [13824, 5120], P('tensor', 'member'), may hold values from -0.0546875 to 0.0546875
- d_table: bfloat16 [128, 3, 4, 5120], P('member'), may hold values from -6 to 6
- f_table: bfloat16 [128, 3, 4, 13824], P('member', None, None, 'tensor'), may hold values from -6 to 6
- seeds: int32 [64], P('member'), may hold values from 0 to 15
- fitness: float32 [64], P('member'), may hold values from -6 to 6
Outputs:
- outputs: bfloat16 [64, 128, 5120], P('member', None, 'tensor')
- delta_gate: bfloat16 [5120, 13824], P('member', 'tensor')
- delta_up: bfloat16 [5120, 13824], P('member', 'tensor')
- delta_down: bfloat16 [13824, 5120], P('tensor', 'member')
Inputs may be any that keep to these rules, and one draw needn't show every extreme that they name: Member m uses row (m // 8) * 16 + seeds[m] of both tables, a row in its own group's block.
All inputs are finite; a program needn't handle non-finite values.
Results may differ from a plain program's by a relative error of at most 0.025.
Values may be sent and summed in bfloat16 or wider, within the bound.
No kernel may reach another device: no remote copies, remote signals or barrier semaphores. Data moves between devices by JAX's collectives and lax.ppermute only.
A program may use at most 192 MiB of HBM per device.

v0:
```python
import math
import jax
import jax.numpy as jnp
from jax import lax
from jax.sharding import PartitionSpec as P

D = 5120
FFW = 13824
perturb_gain = 0.5


def shards(prompt_acts, gate_weight, up_weight, down_weight, d_table, f_table, seeds, fitness):
    members = seeds.shape[0]
    prompt_len = prompt_acts.shape[0]
    rank_size = d_table.shape[2]
    d_sel = jnp.take(d_table, seeds, axis=0)
    selected_factors = jnp.take(f_table, seeds, axis=0)
    d_slices = lax.all_to_all(d_sel, "member", split_axis=3, concat_axis=0, tiled=True)
    f_all, fit_all = (
        lax.all_gather(selected_factors, "member", axis=0, tiled=True),
        lax.all_gather(fitness.astype(jnp.bfloat16), "member", axis=0, tiled=True).astype(
            fitness.dtype
        ),
    )
    population = fit_all.shape[0]
    gate_part = jnp.dot(prompt_acts, gate_weight, preferred_element_type=jnp.float32)
    up_part = jnp.dot(prompt_acts, up_weight, preferred_element_type=jnp.float32)
    prompt_full = lax.all_gather(prompt_acts, "member", axis=1, tiled=True)
    gate_sum, up_sum = (
        lax.psum(gate_part.astype(jnp.bfloat16), "member").astype(jnp.float32),
        lax.psum(up_part.astype(jnp.bfloat16), "member").astype(jnp.float32),
    )
    in_factors = d_sel[:, :2].reshape(members * 2 * rank_size, D)
    proj_sum = jnp.dot(prompt_full, in_factors.T, preferred_element_type=jnp.float32)
    base_gate = gate_sum.astype(jnp.bfloat16)
    base_up = up_sum.astype(jnp.bfloat16)
    proj_inputs = (
        (proj_sum / math.sqrt(D)).astype(jnp.bfloat16).reshape(prompt_len, members, 2, rank_size)
    )
    perturbed = jnp.einsum(
        "pmkr,mkrf->mkpf", proj_inputs, selected_factors[:, :2], preferred_element_type=jnp.float32
    )
    gate = base_gate.astype(jnp.float32)[None] + perturb_gain * perturbed[:, 0]
    up = base_up.astype(jnp.float32)[None] + perturb_gain * perturbed[:, 1]
    hidden_state = (jax.nn.silu(gate) * up).astype(jnp.bfloat16)
    projection_here = jnp.einsum(
        "cdv,czv->cdz", hidden_state, selected_factors[:, 2], preferred_element_type=jnp.float32
    )
    proj_down = (lax.psum(projection_here, "tensor") / math.sqrt(FFW)).astype(jnp.bfloat16)
    hidden_rows = hidden_state.reshape(members * prompt_len, hidden_state.shape[2])
    partial_value = jnp.dot(
        hidden_rows,
        lax.all_gather(down_weight, "member", axis=1, tiled=True),
        preferred_element_type=jnp.float32,
    )
    summed = lax.psum_scatter(
        partial_value.astype(jnp.bfloat16), "tensor", scatter_dimension=1, tiled=True
    ).astype(jnp.float32)
    local_column_range = summed.shape[1]
    col_start = lax.axis_index("tensor") * local_column_range
    out_factor = lax.dynamic_slice_in_dim(d_sel[:, 2], col_start, local_column_range, 2)
    down_noise_delta = perturb_gain * jnp.einsum(
        "mpr,mrd->mpd", proj_down, out_factor, preferred_element_type=jnp.float32
    )
    outputs = (summed.reshape(members, prompt_len, local_column_range) + down_noise_delta).astype(
        jnp.bfloat16
    )
    mean = jnp.sum(fit_all) / population
    spread = jnp.sum((fit_all - mean) ** 2) / population
    score = (fit_all - mean) / jnp.sqrt(spread + 1.0)
    weighted = (d_slices.astype(jnp.float32) * score[:, None, None, None]).astype(jnp.bfloat16)
    scale = 1.0 / math.sqrt(population * rank_size)
    width_cols = weighted.shape[3]
    hidden_cols = f_all.shape[3]
    w_gate = weighted[:, 0].reshape(population * rank_size, width_cols)
    w_up = weighted[:, 1].reshape(population * rank_size, width_cols)
    w_down = weighted[:, 2].reshape(population * rank_size, width_cols)
    f_gate = f_all[:, 0].reshape(population * rank_size, hidden_cols)
    f_up = f_all[:, 1].reshape(population * rank_size, hidden_cols)
    down_factor_columns = f_all[:, 2].reshape(population * rank_size, hidden_cols)
    delta_gate = (jnp.dot(w_gate.T, f_gate, preferred_element_type=jnp.float32) * scale).astype(
        jnp.bfloat16
    )
    delta_up = (jnp.dot(w_up.T, f_up, preferred_element_type=jnp.float32) * scale).astype(
        jnp.bfloat16
    )
    delta_down = (
        jnp.dot(down_factor_columns.T, w_down, preferred_element_type=jnp.float32) * scale
    ).astype(jnp.bfloat16)
    return (outputs, delta_gate, delta_up, delta_down)


def solution(mesh):
    in_specs = (
        P(None, "member"),
        P("member", "tensor"),
        P("member", "tensor"),
        P("tensor", "member"),
        P("member", None, None, None),
        P("member", None, None, "tensor"),
        P("member"),
        P("member"),
    )
    out_specs = (
        P("member", None, "tensor"),
        P("member", "tensor"),
        P("member", "tensor"),
        P("tensor", "member"),
    )
    return jax.shard_map(shards, mesh=mesh, in_specs=in_specs, out_specs=out_specs, check_vma=False)
```

profile of v0, /device:TPU:0, one launch (start us, length us, event | category | flops | bytes accessed | tf_op | source)
XLA Modules:
  0.0 510.3 jit_solution(4729490581838769242)
XLA Ops:
  7.2 0.0 copy-start
  7.2 0.0 all-reduce.4.cloned.1.call-start
  7.2 4.3 convolution_convert_fusion.1
  11.5 0.0 copy-start.4
  11.5 4.2 convolution_convert_fusion.2
  15.6 0.0 all-reduce.4.cloned.1.call-update
  15.7 0.0 all-gather.4.cloned.1.call-start
  15.7 0.7 all-gather.4.cloned.1.call-update
  16.4 0.0 all-gather.6.cloned.1.call-start
  16.5 0.7 all-gather.6.cloned.1.call-update
  17.2 0.0 all-gather.8.cloned.1.call-start
  17.2 0.0 copy-done.4
  17.2 2.4 gather_fusion.1
  19.7 1.2 broadcast_select_fusion.1
  20.9 0.0 all-gather.8.cloned.1.call-update
  20.9 0.0 reduce-scatter.2.cloned.1.call-start
  21.0 0.0 copy-done
  21.0 2.3 gather_fusion
  23.3 1.8 broadcast_select_fusion
  25.1 0.0 copy-start.2
  25.1 0.2 slice.52
  25.3 1.0 reshape.64
  26.3 52.1 %all-reduce.4.cloned.1.call-done = (bf16[128,3456]{1,0:T(8,128)(2,1)}, bf16[128,3456]{1,0:T(8,128)(2,1)}) async-done(((bf16[128,3456]{1,0:T(8,128)(2,1)}, bf16[128,3456]{1,0:T(8,128)(2,1)}), (bf16[128,3456]{1,0:T(8,128)(2,1)}, bf16[128,3456]{1,0:T(8,128)(2,1)})) %all-reduce.4.cloned.1.call-update) | async-done | bytes 1769488 | tf_op jit(solution)/shard_map/psum | solution.py:31
  78.5 1.3 convert_element_type.69
  79.8 0.0 copy-start.3
  79.8 3.1 convert_element_type.73
  82.9 21.3 %all-gather.4.cloned.1.call-done = bf16[128,5120]{1,0:T(8,128)(2,1)} async-done(((bf16[128,640]{1,0:T(8,128)(2,1)}), bf16[128,5120]{1,0:T(8,128)(2,1)}) %all-gather.4.cloned.1.call-update) | async-done | bytes 1310736 | tf_op jit(solution)/shard_map/all_gather | solution.py:28
  104.2 2.1 fusion.12
  106.2 18.7 %fusion.13 = f32[8,2,128,3456]{3,2,1,0:T(8,128)} fusion(bf16[128,8,2,4]{0,3,2,1:T(4,128)(2,1)S(1)} %bitcast.104, bf16[8,3,4,3456]{3,2,1,0:T(4,128)(2,1)} %broadcast_select_fusion.1), kind=kOutput, calls=%fused_computation.34 | convolution fusion | flops 56623104 | bytes 28770304 | tf_op jit(solution)/shard_map/pmkr,mkrf->mkpf/dot_general | solution.py:40
  125.0 11.1 %fusion = f32[8,1,128,3456]{3,2,0,1:T(8,128)} fusion(f32[8,2,128,3456]{3,2,1,0:T(8,128)} %fusion.13), kind=kLoop, calls=%fused_computation.4 | loop fusion | flops 3538944 | bytes 28311552 | tf_op jit(solution)/shard_map/mul | solution.py:43
  136.1 11.2 %slice_multiply_fusion = f32[8,1,128,3456]{3,2,1,0:T(8,128)} fusion(f32[8,2,128,3456]{3,2,1,0:T(8,128)} %fusion.13), kind=kLoop, calls=%fused_computation.2 | loop fusion | flops 3538944 | bytes 28311552 | tf_op jit(solution)/shard_map/mul | solution.py:44
  147.2 0.0 copy-done.3
  147.3 13.3 %fusion.4 = bf16[1024,3456]{1,0:T(8,128)(2,1)} fusion(f32[8,1,128,3456]{3,2,1,0:T(8,128)} %slice_multiply_fusion, f32[8,1,128,3456]{3,2,0,1:T(8,128)} %fusion, f32[128,3456]{1,0:T(8,128)} %convert_element_type.73, f32[128,3456]{1,0:T(8,128)S(1)} %convert_element_type.69), kind=kLoop, calls=%fused_computation.11 | loop fusion | flops 28311552 | bytes 38928384 | tf_op jit(solution)/shard_map/convert_element_type | solution.py:45
  160.6 114.7 %all-gather.6.cloned.1.call-done = bf16[3456,5120]{1,0:T(8,128)(2,1)} async-done(((bf16[3456,640]{1,0:T(8,128)(2,1)}), bf16[3456,5120]{1,0:T(8,128)(2,1)}) %all-gather.6.cloned.1.call-update) | async-done | bytes 35389456 | tf_op jit(solution)/shard_map/all_gather | solution.py:53
  275.2 45.1 %convolution_convert_fusion = bf16[1024,5120]{1,0:T(8,128)(2,1)} fusion(bf16[1024,3456]{1,0:T(8,128)(2,1)} %fusion.4, bf16[3456,5120]{1,0:T(8,128)(2,1)} %all-gather.6.cloned.1.call-done), kind=kOutput, calls=%fused_computation.13 | convolution fusion | flops 36244029440 | bytes 52953088 | tf_op jit(solution)/shard_map/dot_general | solution.py:51
  320.4 0.0 reduce-scatter.2.cloned.1.call-update
  320.4 14.9 %copy.34 = bf16[8,3,4,5120]{0,2,1,3:T(4,128)(2,1)} copy(bf16[8,3,4,5120]{3,2,1,0:T(4,128)(2,1)S(1)} %broadcast_select_fusion) | data formatting | bytes 1966080 | tf_op jit(solution)/shard_map/jit(_take)/select_n | solution.py:16
  335.3 0.0 copy-start.5
  335.3 0.0 copy-start.6
  335.3 19.3 %reshape.104 = bf16[8,2,30720]{2,1,0:T(2,128)(2,1)} reshape(bf16[5120,3,4,8]{3,2,1,0:T(4,128)(2,1)} %bitcast.102) | data formatting | bytes 1966080
  354.6 3.6 all-to-all-start
  358.2 0.0 copy-done.2
  358.2 0.0 copy-done.5
  358.2 0.0 copy-done.6
  358.2 0.7 dynamic-slice.1
  359.5 0.2 dynamic-update-slice
  359.8 19.9 %all-reduce = bf16[64]{0:T(256)(128)(2,1)S(1)} all-reduce(bf16[64]{0:T(256)(128)(2,1)S(1)} %dynamic-update-slice), channel_id=1, replica_groups=mesh['member'=8,'tensor'=4] {'member'}, use_global_device_ids=true, to_apply=%add | all-reduce | flops 64 | bytes 256
  379.7 0.7 convert_reduce_fusion
  381.0 0.7 multiply_reduce_fusion
  382.3 0.0 all-to-all-done
  382.3 19.7 %reshape.105 = bf16[5120,3,4,8]{3,2,1,0:T(4,128)(2,1)} reshape(bf16[8,2,30720]{2,1,0:T(2,128)(2,1)S(1)} %all-to-all-done) | data formatting | bytes 1966080
  402.1 19.0 %copy.35 = f32[8,3,4,8,640]{4,0,3,2,1:T(8,128)S(1)} copy(bf16[8,3,4,8,640]{0,2,1,4,3:T(4,128)(2,1)} %bitcast.101) | data formatting | bytes 2949120 | tf_op jit(solution)/shard_map/convert_element_type | solution.py:71
  421.1 0.2 fusion.11
  421.4 13.1 %fusion.8 = f32[8,128,4]{1,2,0:T(4,128)S(1)} fusion(f32[128,3456]{1,0:T(8,128)} %convert_element_type.73, f32[128,3456]{1,0:T(8,128)} %copy-done.3, bf16[8,3,4,3456]{3,2,1,0:T(4,128)(2,1)} %broadcast_select_fusion.1, f32[8,2,128,3456]{3,2,1,0:T(8,128)} %fusion.13), kind=kOutput, calls=%fused_computation.20 | convolution fusion | flops 63700992 | bytes 32088064 | tf_op jit(solution)/shard_map/cdv,czv->cdz/dot_general | solution.py:46
  434.4 20.0 %psum.23 = f32[8,128,4]{1,2,0:T(4,128)S(1)} all-reduce(f32[8,128,4]{1,2,0:T(4,128)S(1)} %fusion.8), channel_id=1, replica_groups=mesh['member'=8,'tensor'=4] {'tensor'}, use_global_device_ids=true, to_apply=%region_3.4 | all-reduce | flops 4096 | bytes 32768 | tf_op jit(solution)/shard_map/psum | solution.py:49
  454.4 0.0 all-gather.8.cloned.1.call-done
  454.4 3.6 fusion.23
  458.1 3.5 fusion.6
  461.5 3.5 fusion.7
  465.0 3.7 fusion.5
  468.7 30.9 %reduce-scatter.2.cloned.1.call-done = bf16[1024,1280]{1,0:T(8,128)(2,1)} async-done(((bf16[1024,5120]{1,0:T(8,128)(2,1)}), bf16[1024,1280]{1,0:T(8,128)(2,1)}) %reduce-scatter.2.cloned.1.call-update) | async-done | bytes 2621456 | tf_op jit(solution)/shard_map/reduce_scatter | solution.py:56
  499.6 0.0 slice-done
  499.6 4.2 fusion.10
  503.8 0.0 copy-done.1
  (8 shorter events, 0.0 us)
Async XLA Ops:
  7.2 13.8 %copy-start = (bf16[16,3,4,5120]{3,2,1,0:T(4,128)(2,1)S(1)}, bf16[16,3,4,5120]{3,2,1,0:T(4,128)(2,1)}, u32[]{:S(2)}) copy-start(bf16[16,3,4,5120]{3,2,1,0:T(4,128)(2,1)} %param.12) | copy-start | bytes 5898244
  7.2 71.3 %all-reduce.4.cloned.1.call-start = ((), (), s32[]{:S(2)}) async-start(), calls=%async_computation.6 | async-start | bytes 3538944 | tf_op jit(solution)/shard_map/psum | solution.py:31
  11.5 5.7 %copy-start.4 = (s32[8]{0:T(128)S(1)}, s32[8]{0:T(128)}, u32[]{:S(2)}) copy-start(s32[8]{0:T(128)} %param.14) | copy-start | bytes 100
  15.7 88.5 %all-gather.4.cloned.1.call-start = ((), (), s32[]{:S(2)}) async-start(), calls=%async_computation.2 | async-start | bytes 1474560 | tf_op jit(solution)/shard_map/all_gather | solution.py:28
  16.4 258.8 %all-gather.6.cloned.1.call-start = ((), (), s32[]{:S(2)}) async-start(), calls=%async_computation.3 | async-start | bytes 39813120 | tf_op jit(solution)/shard_map/all_gather | solution.py:53
  17.2 437.3 %all-gather.8.cloned.1.call-start = ((), (), s32[]{:S(2)}) async-start(), calls=%async_computation.5 | async-start | bytes 5971968 | tf_op jit(solution)/shard_map/all_gather | solution.py:20
  20.9 478.7 %reduce-scatter.2.cloned.1.call-start = ((), (), s32[]{:S(2)}) async-start(), calls=%async_computation.4 | async-start | bytes 13107200 | tf_op jit(solution)/shard_map/reduce_scatter | solution.py:56
  25.1 333.1 %copy-start.2 = (bf16[8,3,4,5120]{3,2,1,0:T(4,128)(2,1)}, bf16[8,3,4,5120]{3,2,1,0:T(4,128)(2,1)S(1)}, u32[]{:S(2)}) copy-start(bf16[8,3,4,5120]{3,2,1,0:T(4,128)(2,1)S(1)} %broadcast_select_fusion) | copy-start | bytes 2949124
  79.8 67.5 %copy-start.3 = (f32[128,3456]{1,0:T(8,128)}, f32[128,3456]{1,0:T(8,128)S(1)}, u32[]{:S(2)}) copy-start(f32[128,3456]{1,0:T(8,128)S(1)} %convert_element_type.69) | copy-start | bytes 5308420
  335.3 22.9 %copy-start.5 = (f32[8]{0:T(128)S(1)}, f32[8]{0:T(128)}, u32[]{:S(2)}) copy-start(f32[8]{0:T(128)} %param.15) | copy-start | bytes 100
  335.3 22.9 %copy-start.6 = (u32[32]{0:T(128)S(1)}, u32[32]{0:T(128)}, u32[]{:S(2)}) copy-start(u32[32]{0:T(128)} %constant.62) | copy-start | bytes 388
  354.6 27.7 %all-to-all-start = ((bf16[8,2,30720]{2,1,0:T(2,128)(2,1)}), bf16[8,2,30720]{2,1,0:T(2,128)(2,1)S(1)}, u32[]{:S(2)}, u32[]{:S(2)}) async-start(bf16[8,2,30720]{2,1,0:T(2,128)(2,1)} %reshape.104), calls=%async_computation.1 | async-start | bytes 1966080 | tf_op jit(solution)/shard_map/all_to_all | solution.py:18
  465.0 34.6 %slice-start = ((bf16[8,3,4,5120]{3,2,1,0:T(4,128)(2,1)}), bf16[8,1,4,5120]{3,2,1,0:T(4,128)(2,1)S(1)}, s32[]{:S(2)}) async-start(bf16[8,3,4,5120]{3,2,1,0:T(4,128)(2,1)} %copy-done.2), calls=%async_computation.7 | async-start | bytes 655360 | tf_op jit(solution)/shard_map/slice | solution.py:61
  465.0 38.8 %copy-start.1 = (bf16[16,3,4,5120]{3,2,1,0:T(4,128)(2,1)S(1)}, bf16[16,3,4,5120]{3,2,1,0:T(4,128)(2,1)}, u32[]{:S(2)}) copy-start(bf16[16,3,4,5120]{3,2,1,0:T(4,128)(2,1)} %param.12) | copy-start | bytes 5898244
Sparse Core Ops, SparseCore 0:
  15.8 62.6 all-reduce.3
  80.4 23.7 all-gather.3
  106.1 169.1 all-gather.5
  277.5 41.2 all-gather.7
  321.1 178.5 reduce-scatter.1
where the time goes:
time: 511 us; the launch traced here: 510 us
  waiting for transfers between devices  220 us (43%)
  matrix products  102 us (20%)
  local copies, waits for them, and re-layouts  83.5 us (16%)
  other arithmetic  44.6 us (9%)
  blocking collectives  39.9 us (8%)
  between operations  15.9 us (3%)
    all_gather x1, waiting for transfers between devices, shards(): lax.all_gather(down_weight, 'member', axis=1, tiled=True)  115 us
    psum x1, waiting for transfers between devices, shards(): lax.psum(up_part.astype(jnp.bfloat16), 'member').astype(jnp.float32)  52.1 us
    dot_general x1, matrix products, shards(): jnp.dot(hidden_rows, lax.all_gather(down_weight, 'member', axis=1, tiled=...  45.1 us
    unnamed x19, local copies, waits for them, and re-layouts  40 us
    reduce_scatter x1, waiting for transfers between devices, shards(): lax.psum_scatter(partial_value.astype(jnp.bfloat16), 'tensor', scatter_di...  30.9 us
    all_gather x1, waiting for transfers between devices, shards(): prompt_full = lax.all_gather(prompt_acts, 'member', axis=1, tiled=True)  21.3 us
    psum x1, blocking collectives, shards(): lax.psum(projection_here, 'tensor') / math.sqrt(FFW)  20 us
    unnamed x1, blocking collectives  19.9 us
  transfers between devices with their start and end apart: 6, of which 4 were waited for; matrix products, arithmetic and copies ran while one was open for 43% of the time, Pallas kernels for 0%

commit v1 on v0

--- a/solution.py
+++ b/solution.py
@@ -50,7 +50,7 @@
     hidden_rows = hidden_state.reshape(members * prompt_len, hidden_state.shape[2])
     partial_value = jnp.dot(
         hidden_rows,
-        lax.all_gather(down_weight, "member", axis=1, tiled=True),
+        jnp.concatenate(lax.all_gather(down_weight, "member"), axis=1),
         preferred_element_type=jnp.float32,
     )
     summed = lax.psum_scatter(

time: 511 us -> 555 us (1.086)
  local copies, waits for them, and re-layouts: 83.5 us -> 128 us
  waiting for transfers between devices: 220 us -> 251 us
  other arithmetic: 44.6 us -> 21.5 us
  matrix products: 102 us -> 92.2 us
    reshape x0 -> x1, local copies, waits for them, and re-layouts: none -> 44.8 us  [shards(): jnp.concatenate(lax.all_gather(down_weight, 'member'), axis=1)]
    all_gather x1, waiting for transfers between devices: 115 us -> 137 us  [shards(): lax.all_gather(down_weight, 'member')]
    mul x2 -> x0, other arithmetic: 22.2 us -> none  [the longest x1 11.2 us: shards(): up = base_up.astype(jnp.float32)[None] + perturb_gain * perturbed[:, 1]]
    dot_general x1, matrix products: 13.1 us -> 5.09 us  [shards(): jnp.einsum('cdv,czv->cdz', hidden_state, selected_factors[:, 2], preferre...]
    reduce_scatter x1, waiting for transfers between devices: 30.9 us -> 38.5 us  [shards(): lax.psum_scatter(partial_value.astype(jnp.bfloat16), 'tensor', scatter_di...]
    unnamed x19 -> x23, local copies, waits for them, and re-layouts: 40 us -> 39.9 us
  transfers between devices with their start and end apart: 6 -> 6, of which waited for: 4 -> 4; matrix products, arithmetic and copies ran while one was open for 43% -> 42% of each run, Pallas kernels for 0% -> 0%
where the time goes in v1:
time: 555 us; the launch traced here: 553 us
  waiting for transfers between devices  251 us (45%)
  local copies, waits for them, and re-layouts  128 us (23%)
  matrix products  92.2 us (17%)
  blocking collectives  40.2 us (7%)
  other arithmetic  21.5 us (4%)
  between operations  16 us (3%)
    all_gather x1, waiting for transfers between devices, shards(): lax.all_gather(down_weight, 'member')  137 us
    psum x1, waiting for transfers between devices, shards(): lax.psum(up_part.astype(jnp.bfloat16), 'member').astype(jnp.float32)  52.1 us
    dot_general x1, matrix products, shards(): jnp.dot(hidden_rows, jnp.concatenate(lax.all_gather(down_weight, 'member'...  45.3 us
    reshape x1, local copies, waits for them, and re-layouts, shards(): jnp.concatenate(lax.all_gather(down_weight, 'member'), axis=1)  44.8 us
    unnamed x23, local copies, waits for them, and re-layouts  39.9 us
    reduce_scatter x1, waiting for transfers between devices, shards(): lax.psum_scatter(partial_value.astype(jnp.bfloat16), 'tensor', scatter_di...  38.5 us
    all_gather x1, waiting for transfers between devices, shards(): prompt_full = lax.all_gather(prompt_acts, 'member', axis=1, tiled=True)  21.9 us
    psum x1, blocking collectives, shards(): lax.psum(projection_here, 'tensor') / math.sqrt(FFW)  20.2 us
  transfers between devices with their start and end apart: 6, of which 4 were waited for; matrix products, arithmetic and copies ran while one was open for 42% of the time, Pallas kernels for 0%

profile of v1, /device:TPU:0, one launch (start us, length us, event | category | flops | bytes accessed | tf_op | source)
XLA Modules:
  0.0 553.1 jit_solution(14586947208636333190)
XLA Ops:
  7.2 0.0 copy-start
  7.2 0.0 copy-start.5
  7.2 0.0 all-reduce.4.cloned.1.call-start
  7.2 0.0 copy-start.4
  7.2 4.3 convolution_convert_fusion.1
  11.5 0.0 copy-done.5
  11.5 0.0 copy-done.4
  11.5 1.8 convolution_convert_fusion.2
  13.4 0.0 copy-start.6
  13.4 0.0 all-reduce.4.cloned.1.call-update
  13.4 0.0 all-gather.5.cloned.1.call-start
  13.4 0.7 all-gather.5.cloned.1.call-update
  14.1 0.0 all-gather.9.cloned.1.call-start
  14.2 0.7 all-gather.9.cloned.1.call-update
  14.9 0.0 all-gather.7.cloned.1.call-start
  14.9 0.0 copy-done.6
  15.0 2.4 gather_fusion.1
  17.4 1.2 broadcast_select_fusion.1
  18.6 0.0 all-gather.7.cloned.1.call-update
  18.6 0.0 reduce-scatter.2.cloned.1.call-start
  18.7 0.0 copy-done
  18.7 2.3 gather_fusion
  21.0 1.8 broadcast_select_fusion
  22.8 0.0 copy-start.2
  22.8 0.2 slice.52
  23.0 1.0 reshape.90
  24.0 52.1 %all-reduce.4.cloned.1.call-done = (bf16[128,3456]{1,0:T(8,128)(2,1)}, bf16[128,3456]{1,0:T(8,128)(2,1)}) async-done(((bf16[128,3456]{1,0:T(8,128)(2,1)}, bf16[128,3456]{1,0:T(8,128)(2,1)}), (bf16[128,3456]{1,0:T(8,128)(2,1)}, bf16[128,3456]{1,0:T(8,128)(2,1)})) %all-reduce.4.cloned.1.call-update) | async-done | bytes 1769488 | tf_op jit(solution)/shard_map/psum | solution.py:31
  76.2 1.3 convert_element_type.80
  77.5 2.5 convert_element_type.76
  80.0 21.9 %all-gather.5.cloned.1.call-done = bf16[128,5120]{1,0:T(8,128)(2,1)} async-done(((bf16[128,640]{1,0:T(8,128)(2,1)}), bf16[128,5120]{1,0:T(8,128)(2,1)}) %all-gather.5.cloned.1.call-update) | async-done | bytes 1310736 | tf_op jit(solution)/shard_map/all_gather | solution.py:28
  101.9 2.1 fusion.12
  104.0 0.0 copy-start.3
  104.0 18.9 %fusion.13 = f32[8,2,128,3456]{3,2,1,0:T(8,128)} fusion(bf16[128,8,2,4]{0,3,2,1:T(4,128)(2,1)S(1)} %bitcast.99, bf16[8,3,4,3456]{3,2,1,0:T(4,128)(2,1)} %broadcast_select_fusion.1), kind=kOutput, calls=%fused_computation.31 | convolution fusion | flops 56623104 | bytes 28770304 | tf_op jit(solution)/shard_map/pmkr,mkrf->mkpf/dot_general | solution.py:40
  122.8 0.0 copy-done.3
  122.8 13.3 %fusion.3 = bf16[8,128,3456]{2,1,0:T(8,128)(2,1)} fusion(f32[8,2,128,3456]{3,2,1,0:T(8,128)} %fusion.13, f32[128,3456]{1,0:T(8,128)S(1)} %convert_element_type.80, f32[128,3456]{1,0:T(8,128)S(1)} %copy-done.3), kind=kLoop, calls=%fused_computation.6 | loop fusion | flops 35389440 | bytes 38928384 | tf_op jit(solution)/shard_map/convert_element_type | solution.py:45
  136.1 137.3 %all-gather.9.cloned.1.call-done = bf16[27648,640]{1,0:T(8,128)(2,1)} async-done(((bf16[3456,640]{1,0:T(8,128)(2,1)}), bf16[27648,640]{1,0:T(8,128)(2,1)}) %all-gather.9.cloned.1.call-update) | async-done | bytes 35389456 | tf_op jit(solution)/shard_map/all_gather | solution.py:53
  273.4 44.8 %copy.49 = bf16[3456,8,640]{0,2,1:T(8,128)(2,1)} copy(bf16[3456,8,640]{2,0,1:T(8,128)(2,1)} %bitcast.95) | data formatting | bytes 70778880 | tf_op jit(solution)/shard_map/reshape | solution.py:53
  318.2 45.3 %convolution_convert_fusion = bf16[1024,5120]{1,0:T(8,128)(2,1)} fusion(bf16[1024,3456]{1,0:T(8,128)(2,1)} %bitcast.97, bf16[3456,5120]{0,1:T(8,128)(2,1)} %bitcast.96), kind=kOutput, calls=%fused_computation.11 | convolution fusion | flops 36244029440 | bytes 52953088 | tf_op jit(solution)/shard_map/dot_general | solution.py:51
  363.5 0.0 reduce-scatter.2.cloned.1.call-update
  363.5 14.9 %copy.50 = bf16[8,3,4,5120]{0,2,1,3:T(4,128)(2,1)} copy(bf16[8,3,4,5120]{3,2,1,0:T(4,128)(2,1)S(1)} %broadcast_select_fusion) | data formatting | bytes 1966080 | tf_op jit(solution)/shard_map/jit(_take)/select_n | solution.py:16
  378.4 19.3 %reshape.133 = bf16[8,2,30720]{2,1,0:T(2,128)(2,1)} reshape(bf16[5120,3,4,8]{3,2,1,0:T(4,128)(2,1)} %bitcast.94) | data formatting | bytes 1966080
  397.7 3.6 all-to-all-start
  401.3 0.0 copy-done.2
  401.3 0.0 copy-done.7
  401.4 0.0 copy-done.8
  401.4 0.6 dynamic-slice.1
  402.6 0.2 dynamic-update-slice
  402.9 19.9 %all-reduce = bf16[64]{0:T(256)(128)(2,1)S(1)} all-reduce(bf16[64]{0:T(256)(128)(2,1)S(1)} %dynamic-update-slice), channel_id=1, replica_groups=mesh['member'=8,'tensor'=4] {'member'}, use_global_device_ids=true, to_apply=%add | all-reduce | flops 64 | bytes 256
  422.8 0.6 convert_reduce_fusion
  424.1 0.6 multiply_reduce_fusion
  425.4 0.0 all-to-all-done
  425.4 19.7 %reshape.134 = bf16[5120,3,4,8]{3,2,1,0:T(4,128)(2,1)} reshape(bf16[8,2,30720]{2,1,0:T(2,128)(2,1)S(1)} %all-to-all-done) | data formatting | bytes 1966080
  445.1 19.0 %copy.51 = f32[8,3,4,8,640]{4,0,3,2,1:T(8,128)S(1)} copy(bf16[8,3,4,8,640]{0,2,1,4,3:T(4,128)(2,1)} %bitcast.93) | data formatting | bytes 2949120 | tf_op jit(solution)/shard_map/convert_element_type | solution.py:71
  464.1 0.2 fusion.11
  464.4 5.1 fusion.15
  469.5 20.2 %psum.23 = f32[8,128,4]{1,2,0:T(4,128)S(1)} all-reduce(f32[8,128,4]{1,2,0:T(4,128)S(1)} %fusion.15), channel_id=1, replica_groups=mesh['member'=8,'tensor'=4] {'tensor'}, use_global_device_ids=true, to_apply=%region_3.4 | all-reduce | flops 4096 | bytes 32768 | tf_op jit(solution)/shard_map/psum | solution.py:49
  489.7 3.6 fusion.22
  493.3 3.5 fusion.9
  496.8 3.5 fusion.8
  500.3 3.7 fusion.7
  504.0 38.5 %reduce-scatter.2.cloned.1.call-done = bf16[1024,1280]{1,0:T(8,128)(2,1)} async-done(((bf16[1024,5120]{1,0:T(8,128)(2,1)}), bf16[1024,1280]{1,0:T(8,128)(2,1)}) %reduce-scatter.2.cloned.1.call-update) | async-done | bytes 2621456 | tf_op jit(solution)/shard_map/reduce_scatter | solution.py:56
  542.4 0.0 slice-done
  542.5 4.2 fusion.10
  546.6 0.0 copy-done.1
  (11 shorter events, 0.0 us)
Async XLA Ops:
  7.2 11.5 %copy-start = (bf16[16,3,4,5120]{3,2,1,0:T(4,128)(2,1)S(1)}, bf16[16,3,4,5120]{3,2,1,0:T(4,128)(2,1)}, u32[]{:S(2)}) copy-start(bf16[16,3,4,5120]{3,2,1,0:T(4,128)(2,1)} %param.12) | copy-start | bytes 5898244
  7.2 4.3 copy-start.5
  7.2 69.0 %all-reduce.4.cloned.1.call-start = ((), (), s32[]{:S(2)}) async-start(), calls=%async_computation.6 | async-start | bytes 3538944 | tf_op jit(solution)/shard_map/psum | solution.py:31
  7.2 4.3 copy-start.4
  13.4 1.6 copy-start.6
  13.4 88.5 %all-gather.5.cloned.1.call-start = ((), (), s32[]{:S(2)}) async-start(), calls=%async_computation.2 | async-start | bytes 1474560 | tf_op jit(solution)/shard_map/all_gather | solution.py:28
  14.1 259.3 %all-gather.9.cloned.1.call-start = ((), (), s32[]{:S(2)}) async-start(), calls=%async_computation.5 | async-start | bytes 39813120 | tf_op jit(solution)/shard_map/all_gather | solution.py:53
  14.9 474.8 %all-gather.7.cloned.1.call-start = ((), (), s32[]{:S(2)}) async-start(), calls=%async_computation.4 | async-start | bytes 5971968 | tf_op jit(solution)/shard_map/all_gather | solution.py:20
  18.6 523.8 %reduce-scatter.2.cloned.1.call-start = ((), (), s32[]{:S(2)}) async-start(), calls=%async_computation.3 | async-start | bytes 13107200 | tf_op jit(solution)/shard_map/reduce_scatter | solution.py:56
  22.8 378.5 %copy-start.2 = (bf16[8,3,4,5120]{3,2,1,0:T(4,128)(2,1)}, bf16[8,3,4,5120]{3,2,1,0:T(4,128)(2,1)S(1)}, u32[]{:S(2)}) copy-start(bf16[8,3,4,5120]{3,2,1,0:T(4,128)(2,1)S(1)} %broadcast_select_fusion) | copy-start | bytes 2949124
  104.0 18.9 %copy-start.3 = (f32[128,3456]{1,0:T(8,128)S(1)}, f32[128,3456]{1,0:T(8,128)}, u32[]{:S(2)}) copy-start(f32[128,3456]{1,0:T(8,128)} %convert_element_type.76) | copy-start | bytes 5308420
  378.4 22.9 %copy-start.7 = (f32[8]{0:T(128)S(1)}, f32[8]{0:T(128)}, u32[]{:S(2)}) copy-start(f32[8]{0:T(128)} %param.15) | copy-start | bytes 100
  378.4 22.9 %copy-start.8 = (u32[32]{0:T(128)S(1)}, u32[32]{0:T(128)}, u32[]{:S(2)}) copy-start(u32[32]{0:T(128)} %constant.62) | copy-start | bytes 388
  397.7 27.6 %all-to-all-start = ((bf16[8,2,30720]{2,1,0:T(2,128)(2,1)}), bf16[8,2,30720]{2,1,0:T(2,128)(2,1)S(1)}, u32[]{:S(2)}, u32[]{:S(2)}) async-start(bf16[8,2,30720]{2,1,0:T(2,128)(2,1)} %reshape.133), calls=%async_computation.1 | async-start | bytes 1966080 | tf_op jit(solution)/shard_map/all_to_all | solution.py:18
  500.3 42.2 %slice-start = ((bf16[8,3,4,5120]{3,2,1,0:T(4,128)(2,1)}), bf16[8,1,4,5120]{3,2,1,0:T(4,128)(2,1)S(1)}, s32[]{:S(2)}) async-start(bf16[8,3,4,5120]{3,2,1,0:T(4,128)(2,1)} %copy-done.2), calls=%async_computation.7 | async-start | bytes 655360 | tf_op jit(solution)/shard_map/slice | solution.py:61
  500.3 46.3 %copy-start.1 = (bf16[16,3,4,5120]{3,2,1,0:T(4,128)(2,1)S(1)}, bf16[16,3,4,5120]{3,2,1,0:T(4,128)(2,1)}, u32[]{:S(2)}) copy-start(bf16[16,3,4,5120]{3,2,1,0:T(4,128)(2,1)} %param.12) | copy-start | bytes 5898244
Sparse Core Ops, SparseCore 0:
  13.5 62.6 all-reduce.3
  78.1 23.7 all-gather.4
  103.8 169.5 all-gather.8
  275.7 41.2 all-gather.6
  363.6 178.7 reduce-scatter.1
